TPU v7x, 32 devices: a whole 2x2x4 slice. The times are simulated.
32 devices in a mesh: group: 8 (over z, y), tok: 4 (over x, core).
Axes of the slice: x: 2, y: 2, z: 4, core: 2. Of those that a mesh axis runs over, the one named last changes fastest.
Arguments:
- tokens: bfloat16 [16384, 2048], P(('group', 'tok')), may hold values from -94 to 94
- learning_rates: float32 [2, 16384], P(None, 'group'), may hold values from 0.1 to 1
- channel_gains: float32 [2, 5, 2048], P(None, None, 'tok'), may hold values from 0.3 to 3
- fast_init: float32 [2, 3, 16, 128, 128], P(None, None, 'tok'), may hold values from -0.5 to 0.5
- step_size: float32 [2, 16], P(None, 'tok'), may hold values from 0.05 to 1
- update_table: int32 [2, 8], replicated, may hold values 0 or 1
Outputs:
- mixed: bfloat16 [16384, 2048], P(('group', 'tok'))
All inputs are finite; a program needn't handle non-finite values.
Results may differ from a plain program's by a relative error of at most 0.033.
Values may be sent and summed in bfloat16 or wider, within the bound.
A program may use at most 64 MiB of HBM per device.

v0:
```python
import jax
import jax.numpy as jnp
from jax import lax
from jax.sharding import PartitionSpec as P

NS_STEPS = 5


MUON_A = 3.4445
MUON_B = -4.775
MUON_C = 2.0315
EPSILON = 1e-06


def passed_along(value, axis, by):
    size = lax.axis_size(axis)
    pairs = [(i, i + by) for i in range(size) if 0 <= i + by < size]
    return lax.ppermute(value, axis, pairs)


def orthogonalize(gradient):
    scaling = lax.rsqrt(jnp.sum(gradient * gradient, axis=(-2, -1), keepdims=True) + EPSILON)
    current = gradient * scaling
    for repeat in range(NS_STEPS):
        square = jnp.einsum("...ij,...kj->...ik", current, current, precision=lax.Precision.HIGHEST)
        polynom = MUON_B * square + MUON_C * jnp.einsum(
            "...ij,...jk->...ik", square, square, precision=lax.Precision.HIGHEST
        )
        current = MUON_A * current + jnp.einsum(
            "...ij,...jk->...ik", polynom, current, precision=lax.Precision.HIGHEST
        )
    return current


def layer_group(stream, entering, gain_rows, rates_row, steps_row, update_flag, inverse):
    row_count, channel_count = stream.shape
    heads_n = entering.shape[1]
    head_dim = entering.shape[2]
    normed = stream.astype(jnp.float32) * inverse[:, None] * gain_rows[0]
    queries = (normed * gain_rows[1]).astype(jnp.bfloat16).reshape(row_count, heads_n, head_dim)
    keys_in = (normed * gain_rows[2]).astype(jnp.bfloat16).reshape(row_count, heads_n, head_dim)
    values_in = (normed * gain_rows[3]).astype(jnp.bfloat16).reshape(row_count, heads_n, head_dim)
    rounded = entering.astype(jnp.bfloat16)
    gate_q = jnp.einsum("thi,hij->thj", queries, rounded[0], preferred_element_type=jnp.float32)
    up_q = jnp.einsum("thi,hij->thj", queries, rounded[1], preferred_element_type=jnp.float32)
    hidden_q = (jax.nn.silu(gate_q) * up_q).astype(jnp.bfloat16)
    output = jnp.einsum(
        "thj,hjk->thk", hidden_q, rounded[2], preferred_element_type=jnp.float32
    ).reshape(row_count, channel_count)
    mixed_rows = (stream.astype(jnp.float32) + gain_rows[4] * output).astype(jnp.bfloat16)
    gate_k = jnp.einsum("thi,hij->thj", keys_in, rounded[0], preferred_element_type=jnp.float32)
    up_k = jnp.einsum("thi,hij->thj", keys_in, rounded[1], preferred_element_type=jnp.float32)
    sigmoid_k = jax.nn.sigmoid(gate_k)
    active_k = gate_k * sigmoid_k
    hidden_k = (active_k * up_k).astype(jnp.bfloat16)
    targets = (rates_row[:, None, None] * values_in.astype(jnp.float32)).astype(jnp.bfloat16)
    back_hidden = jnp.einsum(
        "thk,hjk->thj", targets, rounded[2], preferred_element_type=jnp.float32
    )
    back_up = (back_hidden * active_k).astype(jnp.bfloat16)
    back_gate = (back_hidden * up_k * sigmoid_k * (1.0 + gate_k * (1.0 - sigmoid_k))).astype(
        jnp.bfloat16
    )
    grad_gate = jnp.einsum("thi,thj->hij", keys_in, back_gate, preferred_element_type=jnp.float32)
    grad_up = jnp.einsum("thi,thj->hij", keys_in, back_up, preferred_element_type=jnp.float32)
    grad_down = jnp.einsum("thj,thk->hjk", hidden_k, targets, preferred_element_type=jnp.float32)
    direction = orthogonalize(jnp.stack([grad_gate, grad_up, grad_down]))
    moved_state = entering + (update_flag * steps_row)[None, :, None, None] * direction
    norm_before = jnp.sqrt(jnp.sum(entering * entering, axis=2, keepdims=True) + EPSILON)
    norm_after = jnp.sqrt(jnp.sum(moved_state * moved_state, axis=2, keepdims=True) + EPSILON)
    return (mixed_rows, moved_state * (norm_before / norm_after))


def pass_on(outgoing):
    return passed_along(outgoing, "group", 1)


def body(tokens, learning_rates, channel_gains, fast_init, step_size, update_table):
    start_stream = lax.all_to_all(tokens, "tok", split_axis=1, concat_axis=0, tiled=True)
    group_count = lax.axis_size("group")
    group_index = lax.axis_index("group")
    width_all = start_stream.shape[1] * lax.axis_size("tok")
    layer_count = fast_init.shape[0]
    zero_state = jnp.zeros(fast_init.shape[1:], jnp.float32)

    def tick_work(stream, outgoing, layer_now, active, inverse):
        received = pass_on(outgoing)
        initial = lax.dynamic_index_in_dim(fast_init, layer_now, 0, keepdims=False)
        entering = jnp.where(group_index == 0, initial, received)
        gain_rows = lax.dynamic_index_in_dim(channel_gains, layer_now, 0, keepdims=False)
        rates_row = lax.dynamic_index_in_dim(learning_rates, layer_now, 0, keepdims=False)
        steps_row = lax.dynamic_index_in_dim(step_size, layer_now, 0, keepdims=False)
        table_cell = lax.dynamic_slice(
            update_table, (jnp.asarray(layer_now, jnp.int32), group_index), (1, 1)
        )
        update_flag = table_cell[0, 0].astype(jnp.float32)

        def working(operands):
            return layer_group(
                operands[0], operands[1], gain_rows, rates_row, steps_row, update_flag, inverse
            )

        def resting(operands):
            return (operands[0], operands[2])

        return lax.cond(active, working, resting, (stream, entering, outgoing))

    def one_tick(tick_index, loop_state):
        stream, outgoing = loop_state
        layer_raw = tick_index - group_index
        active = (layer_raw >= 0) & (layer_raw < layer_count)
        layer_now = jnp.clip(layer_raw, 0, layer_count - 1)
        widened = stream.astype(jnp.float32)
        totals = lax.psum(jnp.sum(widened * widened, axis=1), "tok")
        inverse = lax.rsqrt(totals / width_all + EPSILON)
        return tick_work(stream, outgoing, layer_now, active, inverse)

    final_stream, last_state = lax.fori_loop(
        0, layer_count + group_count - 1, one_tick, (start_stream, zero_state)
    )
    return lax.all_to_all(final_stream, "tok", split_axis=0, concat_axis=1, tiled=True)


def solution(mesh):
    in_specs = (
        P(("group", "tok"), None),
        P(None, "group"),
        P(None, None, "tok"),
        P(None, None, "tok", None, None),
        P(None, "tok"),
        P(),
    )
    out_specs = P(("group", "tok"), None)
    return jax.shard_map(body, mesh=mesh, in_specs=in_specs, out_specs=out_specs, check_vma=False)
```

profile of v0, /device:TPU:31, one launch (start us, length us, event | category | flops | bytes accessed | tf_op | source)
XLA Modules:
  0.0 797.3 jit_solution(697076841951351439)
XLA Ops:
  0.0 3.9 copy.32
  3.9 4.4 all-to-all-start
  8.4 23.8 %all-to-all-done = bf16[512,4,512]{0,2,1:T(8,128)(2,1)S(1)} async-done(((bf16[512,4,512]{0,2,1:T(8,128)(2,1)}), bf16[512,4,512]{0,2,1:T(8,128)(2,1)S(1)}, u32[]{:S(2)}, u32[]{:S(2)}) %all-to-all-start) | async-done | bytes 2097184 | tf_op jit(solution)/shard_map/all_to_all | solution.py:79
  32.2 2.4 copy.33
  34.5 2.9 copy.34
  38.4 717.1 %while.17 = (s32[]{:T(128)}, bf16[2048,512]{0,1:T(8,128)(2,1)S(1)}, f32[3,4,128,128]{3,2,1,0:T(8,128)}, s32[]{:T(128)}, f32[2,5,512]{2,1,0:T(8,128)S(1)}, /*inde...) while((s32[]{:T(128)}, bf16[2048,512]{0,1:T(8,128)(2,1)S(1)}, ...), condition=%wide.region_8.9_spmd, body=%wide.region_0.8_spmd.sunk | while | flops 7005345280 | bytes 224676816 | solution.py:118
  40.2 5.7 psum.14
  45.9 13.1 %collective-permute-done = f32[3,4,128,128]{3,2,1,0:T(8,128)S(1)} collective-permute-done((f32[3,4,128,128]{3,2,1,0:T(8,128)}, f32[3,4,128,128]{3,2,1,0:T(8,128)S(1)}, u32[]{:S(2)}, u32[]{:S(2)}) %collective-permute-start) | collective-permute-done | bytes 786464 | tf_op jit(solution)/shard_map/while/body/eval_jaxpr/ppermute | solution.py:18
  60.8 6.5 psum.14
  67.3 11.4 %collective-permute-done = f32[3,4,128,128]{3,2,1,0:T(8,128)S(1)} collective-permute-done((f32[3,4,128,128]{3,2,1,0:T(8,128)}, f32[3,4,128,128]{3,2,1,0:T(8,128)S(1)}, u32[]{:S(2)}, u32[]{:S(2)}) %collective-permute-start) | collective-permute-done | bytes 786464 | tf_op jit(solution)/shard_map/while/body/eval_jaxpr/ppermute | solution.py:18
  80.5 7.4 psum.14
  87.9 10.6 %collective-permute-done = f32[3,4,128,128]{3,2,1,0:T(8,128)S(1)} collective-permute-done((f32[3,4,128,128]{3,2,1,0:T(8,128)}, f32[3,4,128,128]{3,2,1,0:T(8,128)S(1)}, u32[]{:S(2)}, u32[]{:S(2)}) %collective-permute-start) | collective-permute-done | bytes 786464 | tf_op jit(solution)/shard_map/while/body/eval_jaxpr/ppermute | solution.py:18
  100.2 8.0 %psum.14 = f32[2048]{0:T(1024)S(1)} all-reduce(f32[2048]{0:T(1024)S(1)} %multiply_reduce_fusion.5), channel_id=1, replica_groups=mesh['group'=8,'tok'=4] {'tok'}, use_global_device_ids=true, to_apply=%region_2.2 | all-reduce | flops 2048 | bytes 16384 | tf_op jit(solution)/shard_map/while/body/eval_jaxpr/psum | solution.py:114
  108.2 9.2 %collective-permute-done = f32[3,4,128,128]{3,2,1,0:T(8,128)S(1)} collective-permute-done((f32[3,4,128,128]{3,2,1,0:T(8,128)}, f32[3,4,128,128]{3,2,1,0:T(8,128)S(1)}, u32[]{:S(2)}, u32[]{:S(2)}) %collective-permute-start) | collective-permute-done | bytes 786464 | tf_op jit(solution)/shard_map/while/body/eval_jaxpr/ppermute | solution.py:18
  119.2 8.8 %psum.14 = f32[2048]{0:T(1024)S(1)} all-reduce(f32[2048]{0:T(1024)S(1)} %multiply_reduce_fusion.5), channel_id=1, replica_groups=mesh['group'=8,'tok'=4] {'tok'}, use_global_device_ids=true, to_apply=%region_2.2 | all-reduce | flops 2048 | bytes 16384 | tf_op jit(solution)/shard_map/while/body/eval_jaxpr/psum | solution.py:114
  128.0 7.5 collective-permute-done
  137.2 9.7 %psum.14 = f32[2048]{0:T(1024)S(1)} all-reduce(f32[2048]{0:T(1024)S(1)} %multiply_reduce_fusion.5), channel_id=1, replica_groups=mesh['group'=8,'tok'=4] {'tok'}, use_global_device_ids=true, to_apply=%region_2.2 | all-reduce | flops 2048 | bytes 16384 | tf_op jit(solution)/shard_map/while/body/eval_jaxpr/psum | solution.py:114
  146.9 5.8 collective-permute-done
  154.4 10.5 %psum.14 = f32[2048]{0:T(1024)S(1)} all-reduce(f32[2048]{0:T(1024)S(1)} %multiply_reduce_fusion.5), channel_id=1, replica_groups=mesh['group'=8,'tok'=4] {'tok'}, use_global_device_ids=true, to_apply=%region_2.2 | all-reduce | flops 2048 | bytes 16384 | tf_op jit(solution)/shard_map/while/body/eval_jaxpr/psum | solution.py:114
  165.0 4.0 collective-permute-done
  170.8 11.4 %psum.14 = f32[2048]{0:T(1024)S(1)} all-reduce(f32[2048]{0:T(1024)S(1)} %multiply_reduce_fusion.5), channel_id=1, replica_groups=mesh['group'=8,'tok'=4] {'tok'}, use_global_device_ids=true, to_apply=%region_2.2 | all-reduce | flops 2048 | bytes 16384 | tf_op jit(solution)/shard_map/while/body/eval_jaxpr/psum | solution.py:114
  182.2 432.5 %collective-permute-done = f32[3,4,128,128]{3,2,1,0:T(8,128)S(1)} collective-permute-done((f32[3,4,128,128]{3,2,1,0:T(8,128)}, f32[3,4,128,128]{3,2,1,0:T(8,128)S(1)}, u32[]{:S(2)}, u32[]{:S(2)}) %collective-permute-start) | collective-permute-done | bytes 786464 | tf_op jit(solution)/shard_map/while/body/eval_jaxpr/ppermute | solution.py:18
  614.7 62.2 %conditional.2 = ((bf16[2048,512]{0,1:T(8,128)(2,1)S(1)}, f32[3,4,128,128]{3,2,1,0:T(8,128)})) conditional(s32[]{:T(128)} %convert_element_type.141, (bf16[2048,512]{0,1:T(8,128)(2,1)S(1)}, f32[3,4,128,128]{3,2,1,0:T(8,128)}) %tuple.63, (bf16[2048,512]{0,1:T(8,128)(2,1)S(1)}, s32[]{:T(128)}, f32[2,5,512]{2,1,0:T(8,128)S(1)}, f32[2048]{0:T(1024)S(1)}, ...), branch_computations={%region_3.3_spmd, %region_4.7_spmd} | conditional | flops 7002199552 | bytes 219409024 | solution.py:106
  614.7 2.6 fusion.6
  619.3 2.8 fusion.50
  622.2 6.7 fusion.27
  628.9 3.3 fusion.7
  632.2 2.8 fusion.51
  635.0 2.9 fusion.49
  637.8 4.1 copy.28
  642.0 6.6 fusion.35
  653.6 2.4 fusion.41
  678.7 10.6 %psum.14 = f32[2048]{0:T(1024)S(1)} all-reduce(f32[2048]{0:T(1024)S(1)} %multiply_reduce_fusion.5), channel_id=1, replica_groups=mesh['group'=8,'tok'=4] {'tok'}, use_global_device_ids=true, to_apply=%region_2.2 | all-reduce | flops 2048 | bytes 16384 | tf_op jit(solution)/shard_map/while/body/eval_jaxpr/psum | solution.py:114
  689.3 4.0 collective-permute-done
  693.3 62.2 %conditional.2 = ((bf16[2048,512]{0,1:T(8,128)(2,1)S(1)}, f32[3,4,128,128]{3,2,1,0:T(8,128)})) conditional(s32[]{:T(128)} %convert_element_type.141, (bf16[2048,512]{0,1:T(8,128)(2,1)S(1)}, f32[3,4,128,128]{3,2,1,0:T(8,128)}) %tuple.63, (bf16[2048,512]{0,1:T(8,128)(2,1)S(1)}, s32[]{:T(128)}, f32[2,5,512]{2,1,0:T(8,128)S(1)}, f32[2048]{0:T(1024)S(1)}, ...), branch_computations={%region_3.3_spmd, %region_4.7_spmd} | conditional | flops 7002199552 | bytes 219409024 | solution.py:106
  693.3 2.6 fusion.6
  697.9 2.8 fusion.50
  700.7 6.7 fusion.27
  707.5 3.3 fusion.7
  710.7 2.8 fusion.51
  713.6 2.9 fusion.49
  716.4 4.1 copy.28
  720.5 6.6 fusion.35
  732.2 2.4 fusion.41
  755.5 2.5 copy.36
  758.0 33.1 %all_to_all.38 = bf16[4,512,512]{2,1,0:T(8,128)(2,1)S(1)} all-to-all(bf16[4,512,512]{2,1,0:T(8,128)(2,1)} %bitcast.167), channel_id=1, replica_groups=mesh['group'=8,'tok'=4] {'tok'}, dimensions={0} | all-to-all | bytes 4194304 | tf_op jit(solution)/shard_map/all_to_all | solution.py:121
  791.1 2.4 copy.37
  793.4 3.9 copy.38
  (123 shorter events, 70.9 us)
Async XLA Ops:
  0.0 8.3 %copy-start.9 = (f32[2,5,512]{2,0,1:T(2,128)S(1)}, f32[2,5,512]{2,0,1:T(2,128)}, u32[]{:S(2)}) copy-start(f32[2,5,512]{2,0,1:T(2,128)} %param.12) | copy-start | bytes 61444
  3.9 28.2 %all-to-all-start = ((bf16[512,4,512]{0,2,1:T(8,128)(2,1)}), bf16[512,4,512]{0,2,1:T(8,128)(2,1)S(1)}, u32[]{:S(2)}, u32[]{:S(2)}) async-start(bf16[512,4,512]{0,2,1:T(8,128)(2,1)} %bitcast.165), calls=%async_computation | async-start | bytes 4194304 | tf_op jit(solution)/shard_map/all_to_all | solution.py:79
  8.3 30.1 %copy-start.8 = (f32[2,2048]{1,0:T(2,128)S(1)}, f32[2,2048]{1,0:T(2,128)}, u32[]{:S(2)}) copy-start(f32[2,2048]{1,0:T(2,128)} %param.11) | copy-start | bytes 49156
  8.4 30.0 %copy-start.10 = (s32[2,8]{1,0:T(2,128)S(1)}, s32[2,8]{1,0:T(2,128)}, u32[]{:S(2)}) copy-start(s32[2,8]{1,0:T(2,128)} %param.15) | copy-start | bytes 196
  8.4 30.0 %copy-start.11 = (f32[2,4]{1,0:T(2,128)S(1)}, f32[2,4]{1,0:T(2,128)}, u32[]{:S(2)}) copy-start(f32[2,4]{1,0:T(2,128)} %param.14) | copy-start | bytes 100
  38.4 20.6 %collective-permute-start = (f32[3,4,128,128]{3,2,1,0:T(8,128)}, f32[3,4,128,128]{3,2,1,0:T(8,128)S(1)}, u32[]{:S(2)}, u32[]{:S(2)}) collective-permute-start(f32[3,4,128,128]{3,2,1,0:T(8,128)} %get-tuple-element.519), channel_id=1, source_target_pairs={{0,4},{4,8},{8,12},{12,16},{16,20},{20,24},{24,28},{1,5},{5,9},{9,... | collective-permute-start | bytes 2359304 | tf_op jit(solution)/shard_map/while/body/eval_jaxpr/ppermute | solution.py:18
  59.0 19.7 %collective-permute-start = (f32[3,4,128,128]{3,2,1,0:T(8,128)}, f32[3,4,128,128]{3,2,1,0:T(8,128)S(1)}, u32[]{:S(2)}, u32[]{:S(2)}) collective-permute-start(f32[3,4,128,128]{3,2,1,0:T(8,128)} %get-tuple-element.519), channel_id=1, source_target_pairs={{0,4},{4,8},{8,12},{12,16},{16,20},{20,24},{24,28},{1,5},{5,9},{9,... | collective-permute-start | bytes 2359304 | tf_op jit(solution)/shard_map/while/body/eval_jaxpr/ppermute | solution.py:18
  78.8 19.7 %collective-permute-start = (f32[3,4,128,128]{3,2,1,0:T(8,128)}, f32[3,4,128,128]{3,2,1,0:T(8,128)S(1)}, u32[]{:S(2)}, u32[]{:S(2)}) collective-permute-start(f32[3,4,128,128]{3,2,1,0:T(8,128)} %get-tuple-element.519), channel_id=1, source_target_pairs={{0,4},{4,8},{8,12},{12,16},{16,20},{20,24},{24,28},{1,5},{5,9},{9,... | collective-permute-start | bytes 2359304 | tf_op jit(solution)/shard_map/while/body/eval_jaxpr/ppermute | solution.py:18
  98.5 18.9 %collective-permute-start = (f32[3,4,128,128]{3,2,1,0:T(8,128)}, f32[3,4,128,128]{3,2,1,0:T(8,128)S(1)}, u32[]{:S(2)}, u32[]{:S(2)}) collective-permute-start(f32[3,4,128,128]{3,2,1,0:T(8,128)} %get-tuple-element.519), channel_id=1, source_target_pairs={{0,4},{4,8},{8,12},{12,16},{16,20},{20,24},{24,28},{1,5},{5,9},{9,... | collective-permute-start | bytes 2359304 | tf_op jit(solution)/shard_map/while/body/eval_jaxpr/ppermute | solution.py:18
  117.4 18.1 %collective-permute-start = (f32[3,4,128,128]{3,2,1,0:T(8,128)}, f32[3,4,128,128]{3,2,1,0:T(8,128)S(1)}, u32[]{:S(2)}, u32[]{:S(2)}) collective-permute-start(f32[3,4,128,128]{3,2,1,0:T(8,128)} %get-tuple-element.519), channel_id=1, source_target_pairs={{0,4},{4,8},{8,12},{12,16},{16,20},{20,24},{24,28},{1,5},{5,9},{9,... | collective-permute-start | bytes 2359304 | tf_op jit(solution)/shard_map/while/body/eval_jaxpr/ppermute | solution.py:18
  135.5 17.2 %collective-permute-start = (f32[3,4,128,128]{3,2,1,0:T(8,128)}, f32[3,4,128,128]{3,2,1,0:T(8,128)S(1)}, u32[]{:S(2)}, u32[]{:S(2)}) collective-permute-start(f32[3,4,128,128]{3,2,1,0:T(8,128)} %get-tuple-element.519), channel_id=1, source_target_pairs={{0,4},{4,8},{8,12},{12,16},{16,20},{20,24},{24,28},{1,5},{5,9},{9,... | collective-permute-start | bytes 2359304 | tf_op jit(solution)/shard_map/while/body/eval_jaxpr/ppermute | solution.py:18
  152.7 16.4 %collective-permute-start = (f32[3,4,128,128]{3,2,1,0:T(8,128)}, f32[3,4,128,128]{3,2,1,0:T(8,128)S(1)}, u32[]{:S(2)}, u32[]{:S(2)}) collective-permute-start(f32[3,4,128,128]{3,2,1,0:T(8,128)} %get-tuple-element.519), channel_id=1, source_target_pairs={{0,4},{4,8},{8,12},{12,16},{16,20},{20,24},{24,28},{1,5},{5,9},{9,... | collective-permute-start | bytes 2359304 | tf_op jit(solution)/shard_map/while/body/eval_jaxpr/ppermute | solution.py:18
  169.0 445.6 %collective-permute-start = (f32[3,4,128,128]{3,2,1,0:T(8,128)}, f32[3,4,128,128]{3,2,1,0:T(8,128)S(1)}, u32[]{:S(2)}, u32[]{:S(2)}) collective-permute-start(f32[3,4,128,128]{3,2,1,0:T(8,128)} %get-tuple-element.519), channel_id=1, source_target_pairs={{0,4},{4,8},{8,12},{12,16},{16,20},{20,24},{24,28},{1,5},{5,9},{9,... | collective-permute-start | bytes 2359304 | tf_op jit(solution)/shard_map/while/body/eval_jaxpr/ppermute | solution.py:18
  614.7 2.7 copy-start.6
  614.7 2.7 copy-start.7
  617.4 2.0 copy-start.3
  628.9 3.3 copy-start
  642.0 6.6 copy-start.2
  648.6 1.6 copy-start.1
  648.6 2.8 copy-start.5
  651.4 2.2 copy-start.4
  676.9 16.3 %collective-permute-start = (f32[3,4,128,128]{3,2,1,0:T(8,128)}, f32[3,4,128,128]{3,2,1,0:T(8,128)S(1)}, u32[]{:S(2)}, u32[]{:S(2)}) collective-permute-start(f32[3,4,128,128]{3,2,1,0:T(8,128)} %get-tuple-element.519), channel_id=1, source_target_pairs={{0,4},{4,8},{8,12},{12,16},{16,20},{20,24},{24,28},{1,5},{5,9},{9,... | collective-permute-start | bytes 2359304 | tf_op jit(solution)/shard_map/while/body/eval_jaxpr/ppermute | solution.py:18
  693.3 2.7 copy-start.6
  693.3 2.7 copy-start.7
  695.9 2.0 copy-start.3
  707.4 3.3 copy-start
  720.5 6.6 copy-start.2
  727.1 1.6 copy-start.1
  727.2 2.8 copy-start.5
  730.0 2.2 copy-start.4
where the time goes:
time: 800 us; the launch traced here: 797 us
  waiting for transfers between devices  522 us (65%)
  blocking collectives  112 us (14%)
  matrix products  90 us (11%)
  local copies, waits for them, and re-layouts  33.6 us (4%)
  other arithmetic  22.1 us (3%)
  starting transfers between devices  15.9 us (2%)
    ppermute x9, waiting for transfers between devices, passed_along(): return lax.ppermute(value, axis, pairs)  498 us
    psum x9, blocking collectives, one_tick(): totals = lax.psum(jnp.sum(widened * widened, axis=1), 'tok')  78.7 us
    all_to_all x1, blocking collectives, body(): lax.all_to_all(final_stream, 'tok', split_axis=0, concat_axis=1, tiled=True)  33.1 us
    all_to_all x1, waiting for transfers between devices, body(): lax.all_to_all(tokens, 'tok', split_axis=1, concat_axis=0, tiled=True)  23.8 us
    dot_general x10, matrix products, orthogonalize(): jnp.einsum('...ij,...kj->...ik', current, current, precision=lax.Precisio...  17.7 us
  transfers between devices with their start and end apart: 10, of which 10 were waited for; matrix products, arithmetic and copies ran while one was open for 1% of the time, Pallas kernels for 0%

commit v1 on v0

--- a/solution.py
+++ b/solution.py
@@ -1,6 +1,10 @@
+import functools
+
 import jax
 import jax.numpy as jnp
 from jax import lax
+from jax.experimental import pallas as pl
+from jax.experimental.pallas import tpu as pltpu
 from jax.sharding import PartitionSpec as P
 
 NS_STEPS = 5
@@ -121,6 +125,409 @@
     return lax.all_to_all(final_stream, "tok", split_axis=0, concat_axis=1, tiled=True)
 
 
+MESH = pl.DeviceIdType.MESH
+F32 = jnp.float32
+BF16 = jnp.bfloat16
+NN = (((1,), (0,)), ((), ()))
+NT = (((1,), (1,)), ((), ()))
+TN = (((0,), (0,)), ((), ()))
+
+
+def dot(a, b, dims=NN):
+    return lax.dot_general(a, b, dims, preferred_element_type=F32)
+
+
+def halves(value):
+    high = value.astype(BF16)
+    return high, (value - high.astype(F32)).astype(BF16)
+
+
+def dot3(a, b, dims=NN):
+    a_high, a_low = a
+    b_high, b_low = b
+    return dot(a_high, b_high, dims) + (dot(a_high, b_low, dims) + dot(a_low, b_high, dims))
+
+
+def sigmoid(value):
+    return 0.5 * jnp.tanh(0.5 * value) + 0.5
+
+
+def newton_schulz(current):
+    parts = halves(current)
+    square = dot3(parts, parts, NT)
+    square_parts = halves(square)
+    polynom = MUON_B * square + MUON_C * dot3(square_parts, square_parts)
+    return MUON_A * current + dot3(halves(polynom), parts)
+
+
+def chain_kernel(
+    sizes,
+    tokens,
+    totals,
+    rates,
+    packed,
+    flags,
+    initial,
+    out,
+    xin,
+    xout,
+    squares,
+    sent_squares,
+    rate_rows,
+    params,
+    state,
+    columns,
+    gate_up,
+    down,
+    grad_gu,
+    grad_d,
+    x_recv,
+    x_send,
+    sq_recv,
+    sq_send,
+    rate_recv,
+    rate_send,
+    w_recv,
+    w_send,
+    p_recv,
+    p_send,
+    t_send,
+    s_send,
+    out_recv,
+):
+    groups, toks, layers, heads, owned, rows, width, tile = sizes
+    group_tok = rows * toks
+    per = toks // layers
+    tiles = group_tok // tile
+    tiles_row = rows // tile
+    g = lax.axis_index("group")
+    t = lax.axis_index("tok")
+    me = g * toks + t
+    layer = lax.rem(t, layers)
+    head = g * per + t // layers
+    devices = groups * toks
+
+    def remote(source, target, send, recv, to_g, to_t):
+        return pltpu.make_async_remote_copy(
+            src_ref=source,
+            dst_ref=target,
+            send_sem=send,
+            recv_sem=recv,
+            device_id=(to_g, to_t),
+            device_id_type=MESH,
+        )
+
+    def deliver(source, target, send, recv, to_g, to_t):
+        own = to_g * toks + to_t == me
+
+        @pl.when(own)
+        def _():
+            pltpu.make_async_copy(source, target, recv).start()
+
+        @pl.when(jnp.logical_not(own))
+        def _():
+            remote(source, target, send, recv, to_g, to_t).start()
+
+    def sent(source, send, to_g, to_t):
+        @pl.when(to_g * toks + to_t != me)
+        def _():
+            pltpu.make_async_copy(source, source, send).wait()
+
+    def arrived(target, recv):
+        pltpu.make_async_copy(target, target, recv).wait()
+
+    barrier = pltpu.get_barrier_semaphore()
+
+    @pl.loop(1, devices)
+    def _(step):
+        peer = lax.rem(me + step, devices)
+        pl.semaphore_signal(
+            barrier, inc=1, device_id=(peer // toks, lax.rem(peer, toks)), device_id_type=MESH
+        )
+
+    pl.semaphore_wait(barrier, devices - 1)
+
+    def lane(index, size):
+        return pl.ds(pl.multiple_of(index * size, size), size)
+
+    def param_of(to_t):
+        wanted = g * per + to_t // layers
+        return wanted // owned == t, lax.rem(to_t, layers), lax.rem(wanted, owned)
+
+    for to_t in range(toks):
+        holds, lay, slot = param_of(to_t)
+
+        @pl.when(holds)
+        def _():
+            deliver(initial.at[lay, :, slot], state, w_send.at[to_t], w_recv, g, to_t)
+            deliver(packed.at[lay, slot], params, p_send.at[to_t], p_recv, g, to_t)
+
+    @pl.loop(0, groups)
+    def _(i):
+        to_g = lax.rem(g + i, groups)
+        deliver(rates.at[layer], rate_rows.at[g], rate_send.at[to_g], rate_recv, to_g, t)
+
+    @pl.loop(0, heads)
+    def _(i):
+        h = lax.rem(head + i, heads)
+        to_g, to_t = h // per, lax.rem(h, per) * layers
+        deliver(
+            totals, squares.at[g, 0, :, lane(t, rows)], s_send.at[h], sq_recv.at[g], to_g, to_t
+        )
+
+    @pl.loop(0, heads)
+    def _(i):
+        h = lax.rem(head + i, heads)
+        to_g, to_t = h // per, lax.rem(h, per) * layers
+        deliver(
+            tokens.at[:, lane(h, width)],
+            xin.at[lane(g * toks + t, rows)],
+            t_send.at[h],
+            x_recv.at[g, t],
+            to_g,
+            to_t,
+        )
+
+    arrived(state, w_recv)
+    arrived(params, p_recv)
+    arrived(rate_rows, rate_recv)
+
+    gains = params[...]
+    norm_gain = gains[0:1]
+    query_gain = norm_gain * gains[1:2]
+    key_gain = norm_gain * gains[2:3]
+    value_gain = norm_gain * gains[3:4]
+    out_gain = gains[4:5]
+    step_row = gains[5:6]
+    pick_row = lax.broadcasted_iota(jnp.int32, (16, 2 * width), 0)
+    pick_lane = lax.broadcasted_iota(jnp.int32, (16, 2 * width), 1)
+    spread = jnp.where(pick_row // 2 == pick_lane // width, 1.0, 0.0).astype(BF16)
+    ones_rows = jnp.ones((16, width), BF16)
+
+    @pl.loop(0, groups)
+    def _(c):
+        whole = squares.at[c]
+
+        @pl.when(layer == 0)
+        def _():
+            arrived(squares.at[c, 0], sq_recv.at[c])
+            sent_squares[c] = squares[c, 0]
+
+        @pl.when(layer > 0)
+        def _():
+            arrived(whole, sq_recv.at[c])
+            sent_squares[c] = jnp.sum(squares[c], axis=0)
+
+        inverse = lax.rsqrt(sent_squares[c] / (heads * width) + EPSILON)
+        rate = rate_rows[c]
+        inverse_high = inverse.astype(BF16).astype(F32)
+        rate_high = rate.astype(BF16).astype(F32)
+        at_row = lax.broadcasted_iota(jnp.int32, (16, group_tok), 0)
+        stack = jnp.where(at_row == 0, inverse_high, 0.0)
+        stack = jnp.where(at_row == 1, inverse - inverse_high, stack)
+        stack = jnp.where(at_row == 2, rate_high, stack)
+        stack = jnp.where(at_row == 3, rate - rate_high, stack)
+        columns[...] = dot(stack.astype(BF16), spread, TN)
+
+        gate_up[:, :width] = state[0].astype(BF16)
+        gate_up[:, width:] = state[1].astype(BF16)
+        down[...] = state[2].astype(BF16)
+
+        @pl.loop(0, toks)
+        def _(k):
+            arrived(xin.at[lane(c * toks + k, rows)], x_recv.at[c, k])
+
+            @pl.loop(0, tiles_row)
+            def _(i):
+                at = lane(c * tiles + k * tiles_row + i, tile)
+                here = lane(k * tiles_row + i, tile)
+                stream = xin[at, :].astype(F32)
+                normed = stream * columns[here, :width]
+                queries = (normed * query_gain).astype(BF16)
+                both = dot(queries, gate_up[...])
+                gate = both[:, :width]
+                hidden = (gate * sigmoid(gate) * both[:, width:]).astype(BF16)
+                mixed = (stream + out_gain * dot(hidden, down[...])).astype(BF16)
+                xout[at, :] = mixed
+                wide = mixed.astype(F32)
+                total = dot(ones_rows, (wide * wide).astype(BF16), NT)
+                sent_squares[c, :, here] = total[0:1]
+
+            block = xout.at[lane(c * toks + k, rows)]
+
+            @pl.when(layer < layers - 1)
+            def _():
+                remote(
+                    block,
+                    xin.at[lane(c * toks + k, rows)],
+                    x_send.at[c, k],
+                    x_recv.at[c, k],
+                    g,
+                    t + 1,
+                ).start()
+
+            @pl.when(layer == layers - 1)
+            def _():
+                deliver(block, out.at[:, lane(head, width)], x_send.at[c, k], out_recv, c, k)
+
+        @pl.when(layer < layers - 1)
+        def _():
+            @pl.loop(0, heads)
+            def _(h):
+                remote(
+                    sent_squares.at[c],
+                    squares.at[c, head],
+                    sq_send.at[c],
+                    sq_recv.at[c],
+                    h // per,
+                    lax.rem(h, per) * layers + layer + 1,
+                ).start()
+
+        @pl.when(c < groups - 1)
+        def _():
+            grad_gu[...] = jnp.zeros_like(grad_gu)
+            grad_d[...] = jnp.zeros_like(grad_d)
+
+            @pl.loop(0, tiles)
+            def _(i):
+                at = lane(c * tiles + i, tile)
+                here = lane(i, tile)
+                scale = columns[here, :]
+                normed = xin[at, :].astype(F32) * scale[:, :width]
+                keys = (normed * key_gain).astype(BF16)
+                values = (normed * value_gain).astype(BF16).astype(F32)
+                targets = (values * scale[:, width:]).astype(BF16)
+                both = dot(keys, gate_up[...])
+                back = dot(targets, down[...], NT)
+                gate = both[:, :width]
+                up = both[:, width:]
+                sig = sigmoid(gate)
+                act = gate * sig
+                hidden = (act * up).astype(BF16)
+                back_up = (back * act).astype(BF16)
+                back_gate = (back * up * (sig + act * (1.0 - sig))).astype(BF16)
+                grad_gu[...] += dot(keys, jnp.concatenate([back_gate, back_up], axis=1), TN)
+                grad_d[...] += dot(hidden, targets, TN)
+
+            grads = (grad_gu[:, :width], grad_gu[:, width:], grad_d[...])
+            start = tuple(
+                v * lax.rsqrt(jnp.sum(v * v, axis=(0, 1), keepdims=True) + EPSILON) for v in grads
+            )
+            moves = lax.fori_loop(
+                0, NS_STEPS, lambda _, vs: tuple(newton_schulz(v) for v in vs), start
+            )
+            step = step_row * flags[c]
+            for which in range(3):
+                entering = state[which]
+                moved = entering + step * moves[which]
+                before = jnp.sum(entering * entering, axis=0, keepdims=True) + EPSILON
+                after = jnp.sum(moved * moved, axis=0, keepdims=True) + EPSILON
+                state[which] = moved * (jnp.sqrt(before) * lax.rsqrt(after))
+
+    arrived(out, out_recv)
+
+    for to_t in range(toks):
+        holds, lay, slot = param_of(to_t)
+
+        @pl.when(holds)
+        def _():
+            sent(initial.at[lay, :, slot], w_send.at[to_t], g, to_t)
+            sent(packed.at[lay, slot], p_send.at[to_t], g, to_t)
+
+    @pl.loop(0, groups)
+    def _(to_g):
+        sent(rates.at[layer], rate_send.at[to_g], to_g, t)
+
+        @pl.when(layer < layers - 1)
+        def _():
+            arrived(squares.at[to_g], sq_send.at[to_g])
+
+        @pl.loop(0, toks)
+        def _(k):
+            block = xout.at[lane(to_g * toks + k, rows)]
+
+            @pl.when(layer < layers - 1)
+            def _():
+                arrived(block, x_send.at[to_g, k])
+
+            @pl.when(layer == layers - 1)
+            def _():
+                sent(block, x_send.at[to_g, k], to_g, k)
+
+    @pl.loop(0, heads)
+    def _(h):
+        to_g, to_t = h // per, lax.rem(h, per) * layers
+        sent(totals, s_send.at[h], to_g, to_t)
+        sent(tokens.at[:, lane(h, width)], t_send.at[h], to_g, to_t)
+
+
+def head_body(tokens, learning_rates, channel_gains, fast_init, step_size, update_table):
+    groups, toks = lax.axis_size("group"), lax.axis_size("tok")
+    layers, _, owned, width, _ = fast_init.shape
+    rows, channels = tokens.shape
+    heads = owned * toks
+    group_tok = rows * toks
+    wide = tokens.astype(F32)
+    totals = jnp.sum(wide * wide, axis=1).reshape(1, rows)
+    rates = learning_rates.reshape(layers, 1, group_tok)
+    gains = channel_gains.reshape(layers, 5, owned, width).transpose(0, 2, 1, 3)
+    steps = jnp.broadcast_to(step_size[:, :, None, None], (layers, owned, 3, width))
+    packed = jnp.concatenate([gains, steps], axis=2)
+    layer = lax.rem(lax.axis_index("tok"), layers)
+    flag_row = lax.dynamic_index_in_dim(update_table, layer, 0, keepdims=False).astype(F32)
+    flags = jnp.broadcast_to(flag_row[:, None, None], (groups, 1, width))
+    tile = 256
+    sizes = (groups, toks, layers, heads, owned, rows, width, tile)
+    vmem = pl.BlockSpec(memory_space=pltpu.VMEM)
+    anywhere = pl.BlockSpec(memory_space=pl.ANY)
+    dma = pltpu.SemaphoreType.DMA
+    return pl.pallas_call(
+        functools.partial(chain_kernel, sizes),
+        out_shape=jax.ShapeDtypeStruct((rows, channels), BF16),
+        in_specs=[vmem, vmem, vmem, vmem, vmem, anywhere],
+        out_specs=anywhere,
+        scratch_shapes=[
+            pltpu.VMEM((groups * group_tok, width), BF16),
+            pltpu.VMEM((groups * group_tok, width), BF16),
+            pltpu.VMEM((groups, heads, 1, group_tok), F32),
+            pltpu.VMEM((groups, 1, group_tok), F32),
+            pltpu.VMEM((groups, 1, group_tok), F32),
+            pltpu.VMEM((8, width), F32),
+            pltpu.VMEM((3, width, width), F32),
+            pltpu.VMEM((group_tok, 2 * width), F32),
+            pltpu.VMEM((width, 2 * width), BF16),
+            pltpu.VMEM((width, width), BF16),
+            pltpu.VMEM((width, 2 * width), F32),
+            pltpu.VMEM((width, width), F32),
+            dma((groups, toks)),
+            dma((groups, toks)),
+            dma((groups,)),
+            dma((groups,)),
+            dma,
+            dma((groups,)),
+            dma,
+            dma((toks,)),
+            dma,
+            dma((toks,)),
+            dma((heads,)),
+            dma((heads,)),
+            dma,
+        ],
+        compiler_params=pltpu.CompilerParams(
+            collective_id=0, has_side_effects=True, vmem_limit_bytes=48 * 1024 * 1024
+        ),
+    )(tokens, totals, rates, packed, flags, fast_init)
+
+
+def plan(mesh, tokens, fast_init):
+    groups, toks = mesh.shape["group"], mesh.shape["tok"]
+    layers, _, heads, width, _ = fast_init.shape
+    rows = tokens.shape[0] // (groups * toks)
+    fits = groups * toks == layers * heads and toks % layers == 0 and heads % toks == 0
+    fits = fits and rows % 256 == 0 and width % 128 == 0
+    return head_body if fits and tokens.shape[0] * width <= 4 * 1024 * 1024 else body
+
+
 def solution(mesh):
     in_specs = (
         P(("group", "tok"), None),
@@ -131,4 +538,10 @@
         P(),
     )
     out_specs = P(("group", "tok"), None)
-    return jax.shard_map(body, mesh=mesh, in_specs=in_specs, out_specs=out_specs, check_vma=False)
+    def run(*args):
+        chosen = plan(mesh, args[0], args[3])
+        return jax.shard_map(
+            chosen, mesh=mesh, in_specs=in_specs, out_specs=out_specs, check_vma=False
+        )(*args)
+
+    return run

time: 800 us -> 187 us (0.23)
  waiting for transfers between devices: 522 us -> 0 us
  Pallas kernels: 0 us -> 180 us
  blocking collectives: 112 us -> 0 us
  matrix products: 90 us -> 0 us
  local copies, waits for them, and re-layouts: 33.6 us -> 3.65 us
  other arithmetic: 22.1 us -> 2.92 us
  starting transfers between devices: 15.9 us -> 0 us
    ppermute x9 -> x0, waiting for transfers between devices: 498 us -> none  [passed_along(): return lax.ppermute(value, axis, pairs)]
    pallas_call x0 -> x1, Pallas kernels: none -> 180 us  [head_body(): pl.pallas_call(functools.partial(chain_kernel, sizes), out_shape=jax.Shap...]
    dot_general x46 -> x0, matrix products: 90 us -> none  [the longest x10 17.7 us: orthogonalize(): jnp.einsum('...ij,...kj->...ik', current, current, precision=lax.Precisio...]
    psum x9 -> x0, blocking collectives: 78.7 us -> none  [one_tick(): totals = lax.psum(jnp.sum(widened * widened, axis=1), 'tok')]
    all_to_all x1 -> x0, blocking collectives: 33.1 us -> none  [body(): lax.all_to_all(final_stream, 'tok', split_axis=0, concat_axis=1, tiled=True)]
    all_to_all x1 -> x0, waiting for transfers between devices: 23.8 us -> none  [body(): lax.all_to_all(tokens, 'tok', split_axis=1, concat_axis=0, tiled=True)]
    ppermute x9 -> x0, starting transfers between devices: 11.5 us -> none  [passed_along(): return lax.ppermute(value, axis, pairs)]
    convert_element_type x6 -> x1, other arithmetic: 11.9 us -> 0.83 us  [head_body(): lax.dynamic_index_in_dim(update_table, layer, 0, keepdims=False).astype(F32)]
  transfers between devices with their start and end apart: 10 -> 0, of which waited for: 10 -> 0; matrix products, arithmetic and copies ran while one was open for 1% -> 0% of each run, Pallas kernels for 0% -> 0%
where the time goes in v1:
time: 187 us; the launch traced here: 186 us
  Pallas kernels  180 us (96%)
  local copies, waits for them, and re-layouts  3.65 us (2%)
  other arithmetic  2.92 us (2%)
    pallas_call x1, Pallas kernels, head_body(): pl.pallas_call(functools.partial(chain_kernel, sizes), out_shape=jax.Shap...  180 us

profile of v1, /device:TPU:31, one launch (start us, length us, event | category | flops | bytes accessed | tf_op | source)
XLA Modules:
  0.0 186.5 jit_solution(12845061276598646003)
XLA Ops:
  0.0 0.0 copy-start
  0.0 0.0 copy-start.3
  0.0 0.0 copy-start.2
  0.0 0.8 convert_bitcast_fusion
  0.9 2.1 %multiply_reduce_fusion = f32[512]{0:T(512)S(1)} fusion(bf16[512,2048]{1,0:T(8,128)(2,1)} %tokens.1), kind=kLoop, calls=%fused_computation | loop fusion | flops 3145216 | bytes 2099200 | tf_op jit(solution)/shard_map/reduce_sum | solution.py:471
  2.9 0.1 broadcast_in_dim.5.flags
  3.0 0.7 reshape.19.rates
  3.7 0.0 copy-done.3
  3.7 0.1 broadcast_in_dim.4
  3.8 0.0 copy-done.2
  3.9 0.0 copy-done
  3.9 0.0 copy-start.1
  3.9 1.4 copy-done.1
  5.3 179.8 %shard_map.64 = bf16[512,2048]{1,0:T(8,128)(2,1)S(1)} custom-call(bf16[512,2048]{1,0:T(8,128)(2,1)S(1)} %copy-done, f32[1,512]{1,0:T(1,128)S(1)} %bitcast.8, f32[2,1,2048]{2,1,0:T(1,128)S(1)} %reshape.19.rates, f32[2,4,8,128]{3,2,1,0:T(8,128)S(1)} %pad_maximum_fusion.packed, f32[8,1,128]{2,1,0:T(1,128)S(1)} %broadcast_in_dim.5.flags, ...), custom_call_target="tpu_custom_call" | custom-call | tf_op jit(solution)/shard_map/pallas_call | solution.py:484
  185.1 1.3 copy.11
  (3 shorter events, 0.0 us)
Async XLA Ops:
  0.0 3.9 %copy-start = (bf16[512,2048]{1,0:T(8,128)(2,1)S(1)}, bf16[512,2048]{1,0:T(8,128)(2,1)}, u32[]{:S(2)}) copy-start(bf16[512,2048]{1,0:T(8,128)(2,1)} %tokens.1) | copy-start | bytes 6291460
  0.0 3.7 %copy-start.3 = (f32[2,4]{1,0:T(2,128)S(1)}, f32[2,4]{1,0:T(2,128)}, u32[]{:S(2)}) copy-start(f32[2,4]{1,0:T(2,128)} %param.10) | copy-start | bytes 100
  0.0 3.8 %copy-start.2 = (f32[2,5,512]{2,0,1:T(2,128)S(1)}, f32[2,5,512]{2,0,1:T(2,128)}, u32[]{:S(2)}) copy-start(f32[2,5,512]{2,0,1:T(2,128)} %param.8) | copy-start | bytes 61444
  3.9 1.4 copy-start.1

commit v2 on v1

--- a/solution.py
+++ b/solution.py
@@ -142,28 +142,38 @@
     return high, (value - high.astype(F32)).astype(BF16)
 
 
-def dot3(a, b, dims=NN):
-    a_high, a_low = a
-    b_high, b_low = b
-    return dot(a_high, b_high, dims) + (dot(a_high, b_low, dims) + dot(a_low, b_high, dims))
+def product(a, b):
+    a_high, a_low = halves(a)
+    b_high, b_low = halves(b)
+    left = jnp.concatenate([a_high, a_low], axis=1)
+    above = jnp.concatenate([b_high, b_low], axis=1)
+    below = jnp.concatenate([b_high, jnp.zeros_like(b_low)], axis=1)
+    both = dot(left, jnp.concatenate([above, below], axis=0))
+    return both[:, : b.shape[1]] + both[:, b.shape[1] :]
+
+
+def gram(a):
+    high, low = halves(a)
+    left = jnp.concatenate([high, low], axis=1)
+    above = jnp.concatenate([high, high], axis=1)
+    below = jnp.concatenate([low, jnp.zeros_like(low)], axis=1)
+    both = dot(left, jnp.concatenate([above, below], axis=0), NT)
+    return both[:, : a.shape[0]] + both[:, a.shape[0] :]
 
 
 def sigmoid(value):
     return 0.5 * jnp.tanh(0.5 * value) + 0.5
 
 
-def newton_schulz(current):
-    parts = halves(current)
-    square = dot3(parts, parts, NT)
-    square_parts = halves(square)
-    polynom = MUON_B * square + MUON_C * dot3(square_parts, square_parts)
-    return MUON_A * current + dot3(halves(polynom), parts)
+def newton_schulz(values):
+    squares = [gram(v) for v in values]
+    polynoms = [MUON_B * q + MUON_C * product(q, q) for q in squares]
+    return tuple(MUON_A * v + product(p, v) for p, v in zip(polynoms, values))
 
 
 def chain_kernel(
     sizes,
     tokens,
-    totals,
     rates,
     packed,
     flags,
@@ -176,7 +186,8 @@
     rate_rows,
     params,
     state,
-    columns,
+    totals,
+    stack,
     gate_up,
     down,
     grad_gu,
@@ -272,20 +283,32 @@
         h = lax.rem(head + i, heads)
         to_g, to_t = h // per, lax.rem(h, per) * layers
         deliver(
-            totals, squares.at[g, 0, :, lane(t, rows)], s_send.at[h], sq_recv.at[g], to_g, to_t
-        )
-
-    @pl.loop(0, heads)
-    def _(i):
-        h = lax.rem(head + i, heads)
-        to_g, to_t = h // per, lax.rem(h, per) * layers
-        deliver(
             tokens.at[:, lane(h, width)],
             xin.at[lane(g * toks + t, rows)],
             t_send.at[h],
             x_recv.at[g, t],
             to_g,
             to_t,
+        )
+
+    ones_rows = jnp.ones((16, width), BF16)
+
+    def sums_of(values):
+        wide = values.astype(F32)
+        return dot(ones_rows, (wide * wide).astype(BF16), NT)[0:1]
+
+    totals[...] = jnp.zeros_like(totals)
+
+    @pl.loop(0, heads)
+    def _(h):
+        totals[...] += sums_of(tokens[:, lane(h, width)])
+
+    @pl.loop(0, heads)
+    def _(i):
+        h = lax.rem(head + i, heads)
+        to_g, to_t = h // per, lax.rem(h, per) * layers
+        deliver(
+            totals, squares.at[g, 0, :, lane(t, rows)], s_send.at[h], sq_recv.at[g], to_g, to_t
         )
 
     arrived(state, w_recv)
@@ -302,8 +325,6 @@
     pick_row = lax.broadcasted_iota(jnp.int32, (16, 2 * width), 0)
     pick_lane = lax.broadcasted_iota(jnp.int32, (16, 2 * width), 1)
     spread = jnp.where(pick_row // 2 == pick_lane // width, 1.0, 0.0).astype(BF16)
-    ones_rows = jnp.ones((16, width), BF16)
-
     @pl.loop(0, groups)
     def _(c):
         whole = squares.at[c]
@@ -323,36 +344,57 @@
         inverse_high = inverse.astype(BF16).astype(F32)
         rate_high = rate.astype(BF16).astype(F32)
         at_row = lax.broadcasted_iota(jnp.int32, (16, group_tok), 0)
-        stack = jnp.where(at_row == 0, inverse_high, 0.0)
-        stack = jnp.where(at_row == 1, inverse - inverse_high, stack)
-        stack = jnp.where(at_row == 2, rate_high, stack)
-        stack = jnp.where(at_row == 3, rate - rate_high, stack)
-        columns[...] = dot(stack.astype(BF16), spread, TN)
+        fill = jnp.where(at_row == 0, inverse_high, 0.0)
+        fill = jnp.where(at_row == 1, inverse - inverse_high, fill)
+        fill = jnp.where(at_row == 2, rate_high, fill)
+        stack[...] = jnp.where(at_row == 3, rate - rate_high, fill).astype(BF16)
 
         gate_up[:, :width] = state[0].astype(BF16)
         gate_up[:, width:] = state[1].astype(BF16)
         down[...] = state[2].astype(BF16)
 
-        @pl.loop(0, toks)
-        def _(k):
-            arrived(xin.at[lane(c * toks + k, rows)], x_recv.at[c, k])
-
-            @pl.loop(0, tiles_row)
-            def _(i):
-                at = lane(c * tiles + k * tiles_row + i, tile)
-                here = lane(k * tiles_row + i, tile)
+        def read(i):
+            at = lane(c * tiles + i, tile)
+            here = lane(i, tile)
+
+            def query():
                 stream = xin[at, :].astype(F32)
-                normed = stream * columns[here, :width]
+                normed = stream * dot(stack[:, here], spread[:, :width], TN)
                 queries = (normed * query_gain).astype(BF16)
                 both = dot(queries, gate_up[...])
                 gate = both[:, :width]
                 hidden = (gate * sigmoid(gate) * both[:, width:]).astype(BF16)
                 mixed = (stream + out_gain * dot(hidden, down[...])).astype(BF16)
                 xout[at, :] = mixed
-                wide = mixed.astype(F32)
-                total = dot(ones_rows, (wide * wide).astype(BF16), NT)
-                sent_squares[c, :, here] = total[0:1]
-
+                sent_squares[c, :, here] = sums_of(mixed)
+
+            def learn():
+                scale = dot(stack[:, here], spread, TN)
+                normed = xin[at, :].astype(F32) * scale[:, :width]
+                keys = (normed * key_gain).astype(BF16)
+                targets = (normed * value_gain * scale[:, width:]).astype(BF16)
+                both = dot(keys, gate_up[...])
+                back = dot(targets, down[...], NT)
+                gate = both[:, :width]
+                up = both[:, width:]
+                sig = sigmoid(gate)
+                act = gate * sig
+                hidden = (act * up).astype(BF16)
+                back_up = (back * act).astype(BF16)
+                back_gate = (back * up * (sig + act * (1.0 - sig))).astype(BF16)
+                backs = jnp.concatenate([back_gate, back_up], axis=1)
+                return dot(keys, backs, TN), dot(hidden, targets, TN)
+
+            return query, learn
+
+        def answer(k):
+            for i in range(tiles_row):
+                read(k * tiles_row + i)[0]()
+
+        def await_rows(k):
+            arrived(xin.at[lane(c * toks + k, rows)], x_recv.at[c, k])
+
+        def send_rows(k):
             block = xout.at[lane(c * toks + k, rows)]
 
             @pl.when(layer < layers - 1)
@@ -370,52 +412,57 @@
             def _():
                 deliver(block, out.at[:, lane(head, width)], x_send.at[c, k], out_recv, c, k)
 
-        @pl.when(layer < layers - 1)
-        def _():
-            @pl.loop(0, heads)
-            def _(h):
-                remote(
-                    sent_squares.at[c],
-                    squares.at[c, head],
-                    sq_send.at[c],
-                    sq_recv.at[c],
-                    h // per,
-                    lax.rem(h, per) * layers + layer + 1,
-                ).start()
+        def send_squares():
+            @pl.when(layer < layers - 1)
+            def _():
+                @pl.loop(0, heads)
+                def _(h):
+                    remote(
+                        sent_squares.at[c],
+                        squares.at[c, head],
+                        sq_send.at[c],
+                        sq_recv.at[c],
+                        h // per,
+                        lax.rem(h, per) * layers + layer + 1,
+                    ).start()
+
+        @pl.when(c == groups - 1)
+        def _():
+            @pl.loop(0, toks)
+            def _(k):
+                await_rows(k)
+                answer(k)
+                send_rows(k)
+
+            send_squares()
 
         @pl.when(c < groups - 1)
         def _():
             grad_gu[...] = jnp.zeros_like(grad_gu)
             grad_d[...] = jnp.zeros_like(grad_d)
 
-            @pl.loop(0, tiles)
-            def _(i):
-                at = lane(c * tiles + i, tile)
-                here = lane(i, tile)
-                scale = columns[here, :]
-                normed = xin[at, :].astype(F32) * scale[:, :width]
-                keys = (normed * key_gain).astype(BF16)
-                values = (normed * value_gain).astype(BF16).astype(F32)
-                targets = (values * scale[:, width:]).astype(BF16)
-                both = dot(keys, gate_up[...])
-                back = dot(targets, down[...], NT)
-                gate = both[:, :width]
-                up = both[:, width:]
-                sig = sigmoid(gate)
-                act = gate * sig
-                hidden = (act * up).astype(BF16)
-                back_up = (back * act).astype(BF16)
-                back_gate = (back * up * (sig + act * (1.0 - sig))).astype(BF16)
-                grad_gu[...] += dot(keys, jnp.concatenate([back_gate, back_up], axis=1), TN)
-                grad_d[...] += dot(hidden, targets, TN)
+            @pl.loop(0, toks)
+            def _(k):
+                await_rows(k)
+                found = [read(k * tiles_row + i)[1]() for i in range(tiles_row)]
+                grad_gu[...] += sum(f[0] for f in found)
+                grad_d[...] += sum(f[1] for f in found)
 
             grads = (grad_gu[:, :width], grad_gu[:, width:], grad_d[...])
             start = tuple(
                 v * lax.rsqrt(jnp.sum(v * v, axis=(0, 1), keepdims=True) + EPSILON) for v in grads
             )
-            moves = lax.fori_loop(
-                0, NS_STEPS, lambda _, vs: tuple(newton_schulz(v) for v in vs), start
-            )
+
+            def beside(k, values):
+                answer(k)
+                values = newton_schulz(values)
+                send_rows(k)
+                return values
+
+            moves = lax.fori_loop(0, toks, beside, start)
+            send_squares()
+            for _ in range(NS_STEPS - toks):
+                moves = newton_schulz(moves)
             step = step_row * flags[c]
             for which in range(3):
                 entering = state[which]
@@ -467,8 +514,6 @@
     rows, channels = tokens.shape
     heads = owned * toks
     group_tok = rows * toks
-    wide = tokens.astype(F32)
-    totals = jnp.sum(wide * wide, axis=1).reshape(1, rows)
     rates = learning_rates.reshape(layers, 1, group_tok)
     gains = channel_gains.reshape(layers, 5, owned, width).transpose(0, 2, 1, 3)
     steps = jnp.broadcast_to(step_size[:, :, None, None], (layers, owned, 3, width))
@@ -484,7 +529,7 @@
     return pl.pallas_call(
         functools.partial(chain_kernel, sizes),
         out_shape=jax.ShapeDtypeStruct((rows, channels), BF16),
-        in_specs=[vmem, vmem, vmem, vmem, vmem, anywhere],
+        in_specs=[vmem, vmem, vmem, vmem, anywhere],
         out_specs=anywhere,
         scratch_shapes=[
             pltpu.VMEM((groups * group_tok, width), BF16),
@@ -494,7 +539,8 @@
             pltpu.VMEM((groups, 1, group_tok), F32),
             pltpu.VMEM((8, width), F32),
             pltpu.VMEM((3, width, width), F32),
-            pltpu.VMEM((group_tok, 2 * width), F32),
+            pltpu.VMEM((1, rows), F32),
+            pltpu.VMEM((16, group_tok), BF16),
             pltpu.VMEM((width, 2 * width), BF16),
             pltpu.VMEM((width, width), BF16),
             pltpu.VMEM((width, 2 * width), F32),
@@ -516,7 +562,7 @@
         compiler_params=pltpu.CompilerParams(
             collective_id=0, has_side_effects=True, vmem_limit_bytes=48 * 1024 * 1024
         ),
-    )(tokens, totals, rates, packed, flags, fast_init)
+    )(tokens, rates, packed, flags, fast_init)
 
 
 def plan(mesh, tokens, fast_init):
@@ -524,7 +570,7 @@
     layers, _, heads, width, _ = fast_init.shape
     rows = tokens.shape[0] // (groups * toks)
     fits = groups * toks == layers * heads and toks % layers == 0 and heads % toks == 0
-    fits = fits and rows % 256 == 0 and width % 128 == 0
+    fits = fits and toks <= NS_STEPS and rows % 256 == 0 and width % 128 == 0
     return head_body if fits and tokens.shape[0] * width <= 4 * 1024 * 1024 else body
 
 

time: 187 us -> 179 us (0.957)
  Pallas kernels: 180 us -> 171 us
  local copies, waits for them, and re-layouts: 3.65 us -> 6.64 us
  other arithmetic: 2.92 us -> 0.7 us
    pallas_call x1, Pallas kernels: 180 us -> 171 us  [head_body(): pl.pallas_call(functools.partial(chain_kernel, sizes), out_shape=jax.Shap...]
    reduce_sum x1 -> x0, other arithmetic: 2.07 us -> none  [head_body(): totals = jnp.sum(wide * wide, axis=1).reshape(1, rows)]
    unnamed x9 -> x5, local copies, waits for them, and re-layouts: 2.74 us -> 4.32 us
where the time goes in v2:
time: 179 us; the launch traced here: 178 us
  Pallas kernels  171 us (96%)
  local copies, waits for them, and re-layouts  6.64 us (4%)
    pallas_call x1, Pallas kernels, head_body(): pl.pallas_call(functools.partial(chain_kernel, sizes), out_shape=jax.Shap...  171 us
    unnamed x5, local copies, waits for them, and re-layouts  4.32 us

profile of v2, /device:TPU:31, one launch (start us, length us, event | category | flops | bytes accessed | tf_op | source)
XLA Modules:
  0.0 178.2 jit_solution(1816602025513342506)
XLA Ops:
  0.0 0.7 convert_bitcast_fusion
  0.7 0.1 broadcast_in_dim.5.flags
  0.8 0.7 reshape.15.rates
  1.5 0.8 broadcast_in_dim.4
  2.2 0.8 reshape.16
  3.0 0.0 copy-start
  3.1 1.6 copy-done
  4.6 0.0 copy-start.1
  4.6 1.4 copy-done.1
  6.0 170.8 %shard_map.64 = bf16[512,2048]{1,0:T(8,128)(2,1)S(1)} custom-call(bf16[512,2048]{1,0:T(8,128)(2,1)S(1)} %copy-done, f32[2,1,2048]{2,1,0:T(1,128)S(1)} %reshape.15.rates, f32[2,4,8,128]{3,2,1,0:T(8,128)S(1)} %pad_maximum_fusion.packed, f32[8,1,128]{2,1,0:T(1,128)S(1)} %broadcast_in_dim.5.flags, f32[2,3,4,128,128]{4,3,2,1,0:T(8,128)S(1)} %copy-done.1), custom_call_target="tpu_custom_call" | custom-call | tf_op jit(solution)/shard_map/pallas_call | solution.py:529
  176.9 1.3 copy.11
  (2 shorter events, 0.0 us)
Async XLA Ops:
  3.0 1.6 copy-start
  4.6 1.4 copy-start.1

commit v3 on v2

--- a/solution.py
+++ b/solution.py
@@ -521,7 +521,7 @@
     layer = lax.rem(lax.axis_index("tok"), layers)
     flag_row = lax.dynamic_index_in_dim(update_table, layer, 0, keepdims=False).astype(F32)
     flags = jnp.broadcast_to(flag_row[:, None, None], (groups, 1, width))
-    tile = 256
+    tile = 512
     sizes = (groups, toks, layers, heads, owned, rows, width, tile)
     vmem = pl.BlockSpec(memory_space=pltpu.VMEM)
     anywhere = pl.BlockSpec(memory_space=pl.ANY)
@@ -570,7 +570,7 @@
     layers, _, heads, width, _ = fast_init.shape
     rows = tokens.shape[0] // (groups * toks)
     fits = groups * toks == layers * heads and toks % layers == 0 and heads % toks == 0
-    fits = fits and toks <= NS_STEPS and rows % 256 == 0 and width % 128 == 0
+    fits = fits and toks <= NS_STEPS and rows % 512 == 0 and width % 128 == 0
     return head_body if fits and tokens.shape[0] * width <= 4 * 1024 * 1024 else body
 
 

time: 179 us -> 173 us (0.966)
  Pallas kernels: 171 us -> 165 us
    pallas_call x1, Pallas kernels: 171 us -> 165 us  [head_body(): pl.pallas_call(functools.partial(chain_kernel, sizes), out_shape=jax.Shap...]
where the time goes in v3:
time: 173 us; the launch traced here: 172 us
  Pallas kernels  165 us (95%)
  local copies, waits for them, and re-layouts  6.64 us (4%)
    pallas_call x1, Pallas kernels, head_body(): pl.pallas_call(functools.partial(chain_kernel, sizes), out_shape=jax.Shap...  165 us
    unnamed x5, local copies, waits for them, and re-layouts  4.32 us

profile of v3, /device:TPU:31, one launch (start us, length us, event | category | flops | bytes accessed | tf_op | source)
XLA Modules:
  0.0 172.4 jit_solution(15588069629654314759)
XLA Ops:
  0.0 0.7 convert_bitcast_fusion
  0.7 0.1 broadcast_in_dim.5.flags
  0.8 0.7 reshape.15.rates
  1.5 0.8 broadcast_in_dim.4
  2.2 0.8 reshape.16
  3.0 0.0 copy-start
  3.1 1.6 copy-done
  4.6 0.0 copy-start.1
  4.6 1.4 copy-done.1
  6.0 165.0 %shard_map.64 = bf16[512,2048]{1,0:T(8,128)(2,1)S(1)} custom-call(bf16[512,2048]{1,0:T(8,128)(2,1)S(1)} %copy-done, f32[2,1,2048]{2,1,0:T(1,128)S(1)} %reshape.15.rates, f32[2,4,8,128]{3,2,1,0:T(8,128)S(1)} %pad_maximum_fusion.packed, f32[8,1,128]{2,1,0:T(1,128)S(1)} %broadcast_in_dim.5.flags, f32[2,3,4,128,128]{4,3,2,1,0:T(8,128)S(1)} %copy-done.1), custom_call_target="tpu_custom_call" | custom-call | tf_op jit(solution)/shard_map/pallas_call | solution.py:529
  171.1 1.3 copy.11
  (2 shorter events, 0.0 us)
Async XLA Ops:
  3.0 1.6 copy-start
  4.6 1.4 copy-start.1
